TPU v7x, 32 devices: a whole 2x2x4 slice. The times are simulated.
32 devices in a mesh: wide: 2 (over x), narrow: 4 (over y, core), depth: 4 (over z).
Axes of the slice: x: 2, y: 2, z: 4, core: 2. Of those that a mesh axis runs over, the one named last changes fastest.
Arguments:
- patch_store: bfloat16 [8, 1024, 4096], P('wide', 'depth'), may hold values from -6 to 6
- w_key: bfloat16 [4096, 1024], P(None, 'narrow'), may hold values from -0.09375 to 0.09375
- w_value: bfloat16 [4096, 1024], P(None, 'narrow'), may hold values from -0.09375 to 0.09375
- key_gain: float32 [128], replicated, may hold values from 0.1 to 1.9
- query_gain: float32 [128], replicated, may hold values from 0.1 to 1.9
- queries: bfloat16 [32, 4096], P('wide', 'narrow'), may hold values from -6 to 6
- owner_table: int32 [8], replicated, may hold values from 0 to 7, each once
- reader_table: int32 [2, 2], replicated, may hold values from 0 to 7
- request_image: int32 [32], P('wide'), may hold values from 0 to 1
- image_tiles: int32 [8], replicated, may hold values from 1 to 4
Outputs:
- context: bfloat16 [32, 4096], P(('wide', 'depth'), 'narrow')
Inputs may be any that keep to these rules, and one draw needn't show every extreme that they name: owner_table is a permutation of the slots. `reader_table`: entries are image ids; a group's list may repeat an image.
All inputs are finite; a program needn't handle non-finite values.
Results may differ from a plain program's by a relative error of at most 0.012.
Values may be sent and summed in bfloat16 or wider, within the bound.
A program may use at most 64 MiB of HBM per device.

v0:
```python
import math
import jax
import jax.numpy as jnp
from jax import lax
from jax.sharding import PartitionSpec as P

HD = 128
TILE_P = 256
epsilon = 1e-05


def rms_scaled(tensor, scaling):
    return tensor / jnp.sqrt(jnp.mean(tensor * tensor, axis=-1, keepdims=True) + epsilon) * scaling


def local(
    patch_store,
    w_key,
    w_value,
    key_gain,
    query_gain,
    queries,
    owner_table,
    reader_table,
    request_image,
    image_tiles,
):
    images_here, rows_here, model_width = patch_store.shape
    kv_cols = w_key.shape[1]
    kv_local = kv_cols // HD
    patch_rows = patch_store.reshape(images_here * rows_here, model_width)
    key_rows = jnp.dot(patch_rows, w_key, preferred_element_type=jnp.float32).reshape(
        images_here, rows_here, kv_local, HD
    )
    key_rows = (
        rms_scaled(key_rows, key_gain)
        .astype(jnp.bfloat16)
        .reshape(images_here, rows_here * kv_cols)
    )
    values = jnp.dot(patch_rows, w_value, preferred_element_type=jnp.float32).astype(jnp.bfloat16)
    values = values.reshape(images_here, rows_here * kv_cols)
    owner_index = lax.axis_index("wide")
    wanted = owner_table[reader_table]
    read_count = reader_table.shape[1]
    batch_here = queries.shape[0]
    group_size = queries.shape[1] // (kv_local * HD)
    normed = rms_scaled(
        queries.astype(jnp.float32).reshape(batch_here, kv_local, group_size, HD), query_gain
    ).astype(jnp.bfloat16)
    row_ids = lax.axis_index("depth") * rows_here + jnp.arange(rows_here, dtype=jnp.int32)
    scale = 1.0 / math.sqrt(HD)
    local_slots = owner_index * images_here + jnp.arange(images_here, dtype=jnp.int32)
    picker = (wanted[:, :, None] == local_slots[None, None, :]).astype(jnp.bfloat16)
    send_keys = jnp.einsum(
        "wrj,jx->wrx", picker, key_rows, preferred_element_type=jnp.float32
    ).astype(jnp.bfloat16)
    send_values = jnp.einsum(
        "wrj,jx->wrx", picker, values, preferred_element_type=jnp.float32
    ).astype(jnp.bfloat16)
    got_keys, got_values = (
        lax.all_to_all(send_keys, "wide", split_axis=0, concat_axis=0, tiled=True),
        lax.all_to_all(send_values, "wide", split_axis=0, concat_axis=0, tiled=True),
    )
    read_keys = jnp.sum(got_keys, axis=0, dtype=jnp.float32).astype(jnp.bfloat16)
    read_values = jnp.sum(got_values, axis=0, dtype=jnp.float32).astype(jnp.bfloat16)
    read_keys = read_keys.reshape(read_count, rows_here, kv_local, HD)
    read_values = read_values.reshape(read_count, rows_here, kv_local, HD)
    scores = (
        jnp.einsum("bkgd,rskd->bkgrs", normed, read_keys, preferred_element_type=jnp.float32)
        * scale
    )
    my_images = reader_table[owner_index]
    chosen = (request_image[:, None] == jnp.arange(read_count, dtype=jnp.int32)[None, :]).astype(
        jnp.float32
    )
    usable = (row_ids[None, :] // TILE_P < image_tiles[my_images][:, None]).astype(jnp.float32)
    weights = jnp.exp(scores) * chosen[:, None, None, :, None] * usable[None, None, None]
    denominator = jnp.sum(weights, axis=(3, 4)).reshape(batch_here, kv_local * group_size)
    numerator = jnp.einsum(
        "bkgrs,rskd->bkgd",
        weights.astype(jnp.bfloat16),
        read_values,
        preferred_element_type=jnp.float32,
    )
    numerator = numerator.reshape(batch_here, kv_local * group_size * HD)
    row_share = batch_here // lax.axis_size("depth")
    numerator, denominator = (
        lax.psum(numerator.astype(jnp.bfloat16), "depth").astype(jnp.float32),
        lax.psum(denominator.astype(jnp.bfloat16), "depth").astype(jnp.float32),
    )
    first_row = lax.axis_index("depth") * row_share
    numerator = lax.dynamic_slice_in_dim(numerator, first_row, row_share, 0)
    denominator = lax.dynamic_slice_in_dim(denominator, first_row, row_share, 0)
    heads_here = denominator.shape[1]
    context = numerator.reshape(row_share, heads_here, HD) / denominator[:, :, None]
    return context.reshape(row_share, heads_here * HD).astype(jnp.bfloat16)


def solution(mesh):
    placed = (
        P("wide", "depth", None),
        P(None, "narrow"),
        P(None, "narrow"),
        P(),
        P(),
        P("wide", "narrow"),
        P(),
        P(),
        P("wide"),
        P(),
    )
    return jax.shard_map(
        local, mesh=mesh, in_specs=placed, out_specs=P(("wide", "depth"), "narrow"), check_vma=False
    )
```

profile of v0, /device:TPU:0, one launch (start us, length us, event | category | flops | bytes accessed | tf_op | source)
XLA Modules:
  0.0 63.2 jit_solution(15374107702283691047)
XLA Ops:
  0.0 0.0 copy-start
  0.0 4.3 %copy.48 = bf16[256,4096]{1,0:T(8,128)(2,1)} copy(bf16[256,4096]{0,1:T(8,128)(2,1)} %bitcast.51) | data formatting | bytes 4194304 | tf_op jit(solution)/shard_map/dot_general | solution.py:32
  4.3 0.0 copy-start.5
  4.3 6.4 %multiply_reduce_fusion = (f32[4,256,2]{1,2,0:T(2,128)S(1)}, f32[4,256,2,128]{1,3,2,0:T(8,128)S(1)}) fusion(bf16[2,128,4096,1]{2,1,0,3:T(8,128)(2,1)} %bitcast.52, bf16[4,256,4096]{2,1,0:T(8,128)(2,1)} %param.10), kind=kOutput, calls=%fused_computation.16 | convolution fusion | flops 2148005888 | bytes 11542528 | tf_op jit(solution)/shard_map/dot_general | solution.py:32
  10.6 0.0 copy-start.4
  10.7 0.0 copy-start.1
  10.7 0.0 copy-done.5
  10.7 0.1 multiply_convert_fusion
  10.8 0.4 copy.32
  11.3 0.0 copy-start.3
  11.3 0.0 copy-start.2
  11.3 0.2 reshape.199
  11.5 0.0 copy-done.4
  11.5 0.1 reshape.180
  11.6 0.0 copy-done.1
  11.6 0.6 %gather_fusion = s32[4]{0:T(128)S(1)} fusion(s32[8]{0:T(128)S(1)} %copy-done.1, s32[1024]{0:T(1024)S(1)} %pad_clamp_fusion.1), kind=kCustom, calls=%fused_computation | custom fusion | bytes 48 | tf_op jit(solution)/shard_map/gather | solution.py:43
  12.2 0.1 reshape.179
  12.3 1.4 %convolution_convert_fusion = bf16[2,2,65536]{2,1,0:T(2,128)(2,1)} fusion(bf16[4,65536,1]{1,0,2:T(4,128)(2,1)S(1)} %reshape.199, s32[4]{0:T(128)S(1)} %iota_add_fusion, s32[2,2]{1,0:T(2,128)S(1)} %reshape.179), kind=kOutput, calls=%fused_computation.2 | convolution fusion | flops 2359312 | bytes 1048608 | tf_op jit(solution)/shard_map/wrj,jx->wrx/dot_general | solution.py:54
  13.7 4.2 %all-to-all-start.1 = ((bf16[2,2,65536]{2,1,0:T(2,128)(2,1)}), bf16[2,2,65536]{2,1,0:T(2,128)(2,1)S(1)}, u32[]{:S(2)}, u32[]{:S(2)}) async-start(bf16[2,2,65536]{2,1,0:T(2,128)(2,1)} %convolution_convert_fusion), calls=%async_computation.1 | async-start | bytes 1048576 | tf_op jit(solution)/shard_map/all_to_all | solution.py:61
  18.0 0.0 copy-done.3
  18.0 0.1 multiply_reduce_fusion.1
  18.1 0.1 copy.33
  18.2 0.0 copy-done.2
  18.2 0.6 %gather_fusion.1 = s32[2]{0:T(128)S(1)} fusion(s32[8]{0:T(128)S(1)} %copy-done.2, s32[1024]{0:T(1024)S(1)} %pad_clamp_fusion), kind=kCustom, calls=%fused_computation.1 | custom fusion | bytes 24 | tf_op jit(solution)/shard_map/gather | solution.py:76
  18.9 0.0 copy-done
  18.9 6.5 %convolution_convert_fusion.2 = bf16[1024,256]{1,0:T(8,128)(2,1)} fusion(bf16[1024,4096]{1,0:T(8,128)(2,1)} %bitcast.56, bf16[4096,256]{1,0:T(8,128)(2,1)S(1)} %copy-done), kind=kOutput, calls=%fused_computation.6 | convolution fusion | flops 2147745792 | bytes 11010048 | tf_op jit(solution)/shard_map/dot_general | solution.py:40
  25.4 0.0 copy-start.7
  25.4 0.1 compare_convert_fusion
  25.5 1.4 %reshape.196 = bf16[4,65536,1]{1,0,2:T(4,128)(2,1)S(1)} reshape(bf16[1024,256]{1,0:T(8,128)(2,1)} %convolution_convert_fusion.2) | data formatting | bytes 1048576 | tf_op jit(solution)/shard_map/reshape | solution.py:41
  26.9 1.4 %convolution_convert_fusion.1 = bf16[2,2,65536]{2,1,0:T(2,128)(2,1)} fusion(bf16[4,65536,1]{1,0,2:T(4,128)(2,1)S(1)} %reshape.196, s32[4]{0:T(128)S(1)} %iota_add_fusion, s32[2,2]{1,0:T(2,128)S(1)} %reshape.179), kind=kOutput, calls=%fused_computation.3 | convolution fusion | flops 2359312 | bytes 1048608 | tf_op jit(solution)/shard_map/wrj,jx->wrx/dot_general | solution.py:57
  28.3 0.0 all-to-all-done.1
  28.3 3.5 %all-to-all-start = ((bf16[2,2,65536]{2,1,0:T(2,128)(2,1)}), bf16[2,2,65536]{2,1,0:T(2,128)(2,1)S(1)}, u32[]{:S(2)}, u32[]{:S(2)}) async-start(bf16[2,2,65536]{2,1,0:T(2,128)(2,1)} %convolution_convert_fusion.1), calls=%async_computation | async-start | bytes 1048576 | tf_op jit(solution)/shard_map/all_to_all | solution.py:62
  31.8 0.0 copy-done.7
  31.8 0.1 copy.34
  31.9 0.0 copy-done.6
  31.9 0.1 fusion.12
  32.0 1.1 %reduce_sum.53 = bf16[2,65536]{1,0:T(2,128)(2,1)S(1)} reduce(bf16[2,2,65536]{2,1,0:T(2,128)(2,1)S(1)} %all-to-all-done.1, bf16[]{:T(256)} %constant.16.clone.1), dimensions={0}, to_apply=%region_2.0 | reduce | flops 131072 | bytes 786434 | tf_op jit(solution)/shard_map/reduce_sum | solution.py:64
  33.2 0.2 reshape.173
  33.4 7.1 %all-to-all-done = bf16[2,2,65536]{2,1,0:T(2,128)(2,1)S(1)} async-done(((bf16[2,2,65536]{2,1,0:T(2,128)(2,1)}), bf16[2,2,65536]{2,1,0:T(2,128)(2,1)S(1)}, u32[]{:S(2)}, u32[]{:S(2)}) %all-to-all-start) | async-done | bytes 524320 | tf_op jit(solution)/shard_map/all_to_all | solution.py:62
  40.5 1.1 %reduce_sum.51 = bf16[2,65536]{1,0:T(2,128)(2,1)S(1)} reduce(bf16[2,2,65536]{2,1,0:T(2,128)(2,1)S(1)} %all-to-all-done, bf16[]{:T(256)} %constant.16.clone.1), dimensions={0}, to_apply=%region_0.0 | reduce | flops 131072 | bytes 786434 | tf_op jit(solution)/shard_map/reduce_sum | solution.py:65
  41.7 0.2 reshape.171
  41.9 0.3 fusion.22
  42.2 0.2 fusion.7
  42.4 19.9 %all-reduce = (bf16[16,8]{0,1:T(8,128)(2,1)S(1)}, bf16[16,1024]{1,0:T(8,128)(2,1)S(1)}) all-reduce(bf16[16,8]{0,1:T(8,128)(2,1)S(1)} %bitcast.55, bf16[16,1024]{1,0:T(8,128)(2,1)S(1)} %convert_element_type.72), channel_id=1, replica_groups=mesh['wide'=2,'narrow'=4,'depth'=4] {'depth'}, use_global_device_ids=true, to_apply=%region_6.7 | all-reduce | flops 16512 | bytes 66048 | tf_op jit(solution)/shard_map/psum | solution.py:89
  62.3 0.1 constant_dynamic-slice_fusion
  62.4 0.1 copy.40
  62.5 0.1 broadcast_bitcast_fusion
  62.6 0.6 fusion.13
  (14 shorter events, 0.1 us)
Async XLA Ops:
  0.0 18.9 %copy-start = (bf16[4096,256]{1,0:T(8,128)(2,1)S(1)}, bf16[4096,256]{1,0:T(8,128)(2,1)}, u32[]{:S(2)}) copy-start(bf16[4096,256]{1,0:T(8,128)(2,1)} %param.12) | copy-start | bytes 6291460
  4.3 6.4 %copy-start.5 = (f32[128]{0:T(128)S(1)}, f32[128]{0:T(128)}, u32[]{:S(2)}) copy-start(f32[128]{0:T(128)} %param.13) | copy-start | bytes 1540
  10.6 0.8 %copy-start.4 = (s32[2,2]{1,0:T(2,128)S(1)}, s32[2,2]{1,0:T(2,128)}, u32[]{:S(2)}) copy-start(s32[2,2]{1,0:T(2,128)} %param.17) | copy-start | bytes 52
  10.7 0.9 %copy-start.1 = (s32[8]{0:T(128)S(1)}, s32[8]{0:T(128)}, u32[]{:S(2)}) copy-start(s32[8]{0:T(128)} %param.16) | copy-start | bytes 100
  11.3 6.7 %copy-start.3 = (bf16[16,1024]{1,0:T(8,128)(2,1)S(1)}, bf16[16,1024]{1,0:T(8,128)(2,1)}, u32[]{:S(2)}) copy-start(bf16[16,1024]{1,0:T(8,128)(2,1)} %param.15) | copy-start | bytes 98308
  11.3 7.0 %copy-start.2 = (s32[8]{0:T(128)S(1)}, s32[8]{0:T(128)}, u32[]{:S(2)}) copy-start(s32[8]{0:T(128)} %param.19) | copy-start | bytes 100
  13.7 14.6 %all-to-all-start.1 = ((bf16[2,2,65536]{2,1,0:T(2,128)(2,1)}), bf16[2,2,65536]{2,1,0:T(2,128)(2,1)S(1)}, u32[]{:S(2)}, u32[]{:S(2)}) async-start(bf16[2,2,65536]{2,1,0:T(2,128)(2,1)} %convolution_convert_fusion), calls=%async_computation.1 | async-start | bytes 1048576 | tf_op jit(solution)/shard_map/all_to_all | solution.py:61
  25.4 6.4 %copy-start.7 = (s32[16]{0:T(128)S(1)}, s32[16]{0:T(128)}, u32[]{:S(2)}) copy-start(s32[16]{0:T(128)} %param.18) | copy-start | bytes 196
  25.4 6.5 %copy-start.6 = (f32[128]{0:T(128)S(1)}, f32[128]{0:T(128)}, u32[]{:S(2)}) copy-start(f32[128]{0:T(128)} %param.14) | copy-start | bytes 1540
  28.3 12.2 %all-to-all-start = ((bf16[2,2,65536]{2,1,0:T(2,128)(2,1)}), bf16[2,2,65536]{2,1,0:T(2,128)(2,1)S(1)}, u32[]{:S(2)}, u32[]{:S(2)}) async-start(bf16[2,2,65536]{2,1,0:T(2,128)(2,1)} %convolution_convert_fusion.1), calls=%async_computation | async-start | bytes 1048576 | tf_op jit(solution)/shard_map/all_to_all | solution.py:62
where the time goes:
time: 63.5 us; the launch traced here: 63.2 us
  blocking collectives  19.9 us (31%)
  matrix products  16.1 us (25%)
  local copies, waits for them, and re-layouts  8.68 us (14%)
  starting transfers between devices  7.75 us (12%)
  waiting for transfers between devices  7.14 us (11%)
  other arithmetic  3.42 us (5%)
    psum x1, blocking collectives, local(): lax.psum(denominator.astype(jnp.bfloat16), 'depth').astype(jnp.float32)  19.9 us
    all_to_all x1, waiting for transfers between devices, local(): lax.all_to_all(send_values, 'wide', split_axis=0, concat_axis=0, tiled=True)  7.14 us
    dot_general x1, matrix products, local(): jnp.dot(patch_rows, w_value, preferred_element_type=jnp.float32)  6.52 us
    dot_general x1, matrix products, local(): jnp.dot(patch_rows, w_key, preferred_element_type=jnp.float32)  6.36 us
    dot_general x1, local copies, waits for them, and re-layouts, local(): jnp.dot(patch_rows, w_key, preferred_element_type=jnp.float32)  4.27 us
    all_to_all x1, starting transfers between devices, local(): lax.all_to_all(send_keys, 'wide', split_axis=0, concat_axis=0, tiled=True)  4.24 us
    all_to_all x1, starting transfers between devices, local(): lax.all_to_all(send_values, 'wide', split_axis=0, concat_axis=0, tiled=True)  3.51 us
    reshape x1, local copies, waits for them, and re-layouts, local(): values = values.reshape(images_here, rows_here * kv_cols)  1.44 us
  transfers between devices with their start and end apart: 2, of which 1 were waited for; matrix products, arithmetic and copies ran while one was open for 19% of the time, Pallas kernels for 0%

commit v1 on v0

--- a/solution.py
+++ b/solution.py
@@ -1,12 +1,21 @@
+import functools
 import math
 import jax
 import jax.numpy as jnp
 from jax import lax
 from jax.sharding import PartitionSpec as P
+from jax.lax import all_gather
 
 HD = 128
 TILE_P = 256
 epsilon = 1e-05
+
+
+def _recast_thing(z, comm_axis):
+    return jnp.sum(all_gather(z, comm_axis), 0)
+
+
+spots_resolve = functools.partial(_recast_thing, comm_axis="depth")
 
 
 def rms_scaled(tensor, scaling):
@@ -86,7 +95,7 @@
     row_share = batch_here // lax.axis_size("depth")
     numerator, denominator = (
         lax.psum(numerator.astype(jnp.bfloat16), "depth").astype(jnp.float32),
-        lax.psum(denominator.astype(jnp.bfloat16), "depth").astype(jnp.float32),
+        spots_resolve(denominator.astype(jnp.bfloat16)).astype(jnp.float32),
     )
     first_row = lax.axis_index("depth") * row_share
     numerator = lax.dynamic_slice_in_dim(numerator, first_row, row_share, 0)

time: 63.5 us -> 67.3 us (1.060)
  blocking collectives: 19.9 us -> 30.6 us
  waiting for transfers between devices: 7.14 us -> 0.01 us
    all_gather x0 -> x1, blocking collectives: none -> 12.9 us  [_recast_thing(): return jnp.sum(all_gather(z, comm_axis), 0)]
    all_to_all x1, waiting for transfers between devices: 7.14 us -> 0.01 us  [local(): lax.all_to_all(send_values, 'wide', split_axis=0, concat_axis=0, tiled=True)]
    psum x1, blocking collectives: 19.9 us -> 17.7 us  [local(): lax.psum(numerator.astype(jnp.bfloat16), 'depth').astype(jnp.float32)]
  transfers between devices with their start and end apart: 2 -> 2, of which waited for: 1 -> 0; matrix products, arithmetic and copies ran while one was open for 19% -> 19% of each run, Pallas kernels for 0% -> 0%
where the time goes in v1:
time: 67.3 us; the launch traced here: 66.9 us
  blocking collectives  30.6 us (45%)
  matrix products  16.1 us (24%)
  local copies, waits for them, and re-layouts  8.7 us (13%)
  starting transfers between devices  7.75 us (12%)
  other arithmetic  3.43 us (5%)
    psum x1, blocking collectives, local(): lax.psum(numerator.astype(jnp.bfloat16), 'depth').astype(jnp.float32)  17.7 us
    all_gather x1, blocking collectives, _recast_thing(): return jnp.sum(all_gather(z, comm_axis), 0)  12.9 us
    dot_general x1, matrix products, local(): jnp.dot(patch_rows, w_value, preferred_element_type=jnp.float32)  6.52 us
    dot_general x1, matrix products, local(): jnp.dot(patch_rows, w_key, preferred_element_type=jnp.float32)  6.36 us
    dot_general x1, local copies, waits for them, and re-layouts, local(): jnp.dot(patch_rows, w_key, preferred_element_type=jnp.float32)  4.27 us
    all_to_all x1, starting transfers between devices, local(): lax.all_to_all(send_keys, 'wide', split_axis=0, concat_axis=0, tiled=True)  4.24 us
    all_to_all x1, starting transfers between devices, local(): lax.all_to_all(send_values, 'wide', split_axis=0, concat_axis=0, tiled=True)  3.51 us
    reshape x1, local copies, waits for them, and re-layouts, local(): values = values.reshape(images_here, rows_here * kv_cols)  1.44 us
  transfers between devices with their start and end apart: 2, of which 0 were waited for; matrix products, arithmetic and copies ran while one was open for 19% of the time, Pallas kernels for 0%

profile of v1, /device:TPU:0, one launch (start us, length us, event | category | flops | bytes accessed | tf_op | source)
XLA Modules:
  0.0 66.9 jit_solution(7649210912033649565)
XLA Ops:
  0.0 0.0 copy-start
  0.0 4.3 %copy.46 = bf16[256,4096]{1,0:T(8,128)(2,1)} copy(bf16[256,4096]{0,1:T(8,128)(2,1)} %bitcast.51) | data formatting | bytes 4194304 | tf_op jit(solution)/shard_map/dot_general | solution.py:41
  4.3 6.4 %multiply_reduce_fusion = (f32[4,256,2]{1,2,0:T(2,128)S(1)}, f32[4,256,2,128]{1,3,2,0:T(8,128)S(1)}) fusion(bf16[2,128,4096,1]{2,1,0,3:T(8,128)(2,1)} %bitcast.52, bf16[4,256,4096]{2,1,0:T(8,128)(2,1)} %param.10), kind=kOutput, calls=%fused_computation.16 | convolution fusion | flops 2148005888 | bytes 11542528 | tf_op jit(solution)/shard_map/dot_general | solution.py:41
  10.6 0.0 copy-start.4
  10.7 0.0 copy-start.1
  10.7 0.0 copy-done.5
  10.7 0.1 multiply_convert_fusion
  10.8 0.4 copy.30
  11.3 0.0 copy-start.3
  11.3 0.0 copy-start.2
  11.3 0.2 reshape.209
  11.5 0.0 copy-done.4
  11.5 0.0 copy-start.6
  11.5 0.1 reshape.190
  11.6 0.0 copy-done.1
  11.6 0.6 gather_fusion
  12.3 0.1 reshape.189
  12.3 1.4 %convolution_convert_fusion = bf16[2,2,65536]{2,1,0:T(2,128)(2,1)} fusion(bf16[4,65536,1]{1,0,2:T(4,128)(2,1)S(1)} %reshape.209, s32[4]{0:T(128)S(1)} %iota_add_fusion, s32[2,2]{1,0:T(2,128)S(1)} %reshape.189), kind=kOutput, calls=%fused_computation.2 | convolution fusion | flops 2359312 | bytes 1048608 | tf_op jit(solution)/shard_map/wrj,jx->wrx/dot_general | solution.py:63
  13.7 4.2 %all-to-all-start.1 = ((bf16[2,2,65536]{2,1,0:T(2,128)(2,1)}), bf16[2,2,65536]{2,1,0:T(2,128)(2,1)S(1)}, u32[]{:S(2)}, u32[]{:S(2)}) async-start(bf16[2,2,65536]{2,1,0:T(2,128)(2,1)} %convolution_convert_fusion), calls=%async_computation.1 | async-start | bytes 1048576 | tf_op jit(solution)/shard_map/all_to_all | solution.py:70
  18.0 0.0 copy-done.3
  18.0 0.1 multiply_reduce_fusion.1
  18.1 0.1 copy.31
  18.2 0.1 copy.32
  18.3 0.0 copy-done.2
  18.3 0.6 gather_fusion.1
  19.0 0.1 compare_convert_fusion
  19.1 0.0 copy-done.6
  19.1 0.1 fusion.12
  19.2 0.0 copy-done
  19.2 0.0 copy-start.7
  19.2 6.5 %convolution_convert_fusion.2 = bf16[1024,256]{1,0:T(8,128)(2,1)} fusion(bf16[1024,4096]{1,0:T(8,128)(2,1)} %bitcast.56, bf16[4096,256]{1,0:T(8,128)(2,1)S(1)} %copy-done), kind=kOutput, calls=%fused_computation.6 | convolution fusion | flops 2147745792 | bytes 11010048 | tf_op jit(solution)/shard_map/dot_general | solution.py:49
  25.7 1.4 %reshape.206 = bf16[4,65536,1]{1,0,2:T(4,128)(2,1)S(1)} reshape(bf16[1024,256]{1,0:T(8,128)(2,1)} %convolution_convert_fusion.2) | data formatting | bytes 1048576 | tf_op jit(solution)/shard_map/reshape | solution.py:50
  27.2 1.4 %convolution_convert_fusion.1 = bf16[2,2,65536]{2,1,0:T(2,128)(2,1)} fusion(bf16[4,65536,1]{1,0,2:T(4,128)(2,1)S(1)} %reshape.206, s32[4]{0:T(128)S(1)} %iota_add_fusion, s32[2,2]{1,0:T(2,128)S(1)} %reshape.189), kind=kOutput, calls=%fused_computation.3 | convolution fusion | flops 2359312 | bytes 1048608 | tf_op jit(solution)/shard_map/wrj,jx->wrx/dot_general | solution.py:66
  28.6 0.0 all-to-all-done.1
  28.6 3.5 %all-to-all-start = ((bf16[2,2,65536]{2,1,0:T(2,128)(2,1)}), bf16[2,2,65536]{2,1,0:T(2,128)(2,1)S(1)}, u32[]{:S(2)}, u32[]{:S(2)}) async-start(bf16[2,2,65536]{2,1,0:T(2,128)(2,1)} %convolution_convert_fusion.1), calls=%async_computation | async-start | bytes 1048576 | tf_op jit(solution)/shard_map/all_to_all | solution.py:71
  32.1 1.1 %reduce_sum.65 = bf16[2,65536]{1,0:T(2,128)(2,1)S(1)} reduce(bf16[2,2,65536]{2,1,0:T(2,128)(2,1)S(1)} %all-to-all-done.1, bf16[]{:T(256)} %constant.42.clone.1), dimensions={0}, to_apply=%region_2.0 | reduce | flops 131072 | bytes 786434 | tf_op jit(solution)/shard_map/reduce_sum | solution.py:73
  33.2 0.2 reshape.183
  33.4 0.3 fusion.22
  33.7 12.9 %all_gather.4 = bf16[4,16,8]{1,2,0:T(8,128)(2,1)S(1)} all-gather(bf16[1,16,8]{1,2,0:T(8,128)(2,1)S(1)} %bitcast.55), channel_id=1, replica_groups=mesh['wide'=2,'narrow'=4,'depth'=4] {'depth'}, dimensions={0}, use_global_device_ids=true | all-gather | bytes 1280 | tf_op jit(solution)/shard_map/all_gather | solution.py:15
  46.7 0.1 constant_dynamic-slice_fusion
  46.7 0.1 copy.38
  46.8 0.1 broadcast_bitcast_fusion
  46.9 0.0 all-to-all-done
  46.9 1.1 %reduce_sum.63 = bf16[2,65536]{1,0:T(2,128)(2,1)S(1)} reduce(bf16[2,2,65536]{2,1,0:T(2,128)(2,1)S(1)} %all-to-all-done, bf16[]{:T(256)} %constant.42.clone.1), dimensions={0}, to_apply=%region_0.0 | reduce | flops 131072 | bytes 786434 | tf_op jit(solution)/shard_map/reduce_sum | solution.py:74
  48.1 0.2 reshape.181
  48.3 0.2 fusion.7
  48.5 17.7 %psum.7 = bf16[16,1024]{1,0:T(8,128)(2,1)S(1)} all-reduce(bf16[16,1024]{1,0:T(8,128)(2,1)S(1)} %convert_element_type.81), channel_id=1, replica_groups=mesh['wide'=2,'narrow'=4,'depth'=4] {'depth'}, use_global_device_ids=true, to_apply=%region_4.5 | all-reduce | flops 16384 | bytes 65536 | tf_op jit(solution)/shard_map/psum | solution.py:97
  66.3 0.6 fusion.13
  (16 shorter events, 0.2 us)
Async XLA Ops:
  0.0 19.2 %copy-start = (bf16[4096,256]{1,0:T(8,128)(2,1)S(1)}, bf16[4096,256]{1,0:T(8,128)(2,1)}, u32[]{:S(2)}) copy-start(bf16[4096,256]{1,0:T(8,128)(2,1)} %param.12) | copy-start | bytes 6291460
  4.3 6.4 %copy-start.5 = (f32[128]{0:T(128)S(1)}, f32[128]{0:T(128)}, u32[]{:S(2)}) copy-start(f32[128]{0:T(128)} %param.13) | copy-start | bytes 1540
  10.6 0.8 %copy-start.4 = (s32[2,2]{1,0:T(2,128)S(1)}, s32[2,2]{1,0:T(2,128)}, u32[]{:S(2)}) copy-start(s32[2,2]{1,0:T(2,128)} %param.17) | copy-start | bytes 52
  10.7 1.0 %copy-start.1 = (s32[8]{0:T(128)S(1)}, s32[8]{0:T(128)}, u32[]{:S(2)}) copy-start(s32[8]{0:T(128)} %param.16) | copy-start | bytes 100
  11.3 6.7 %copy-start.3 = (bf16[16,1024]{1,0:T(8,128)(2,1)S(1)}, bf16[16,1024]{1,0:T(8,128)(2,1)}, u32[]{:S(2)}) copy-start(bf16[16,1024]{1,0:T(8,128)(2,1)} %param.15) | copy-start | bytes 98308
  11.3 7.1 %copy-start.2 = (s32[8]{0:T(128)S(1)}, s32[8]{0:T(128)}, u32[]{:S(2)}) copy-start(s32[8]{0:T(128)} %param.19) | copy-start | bytes 100
  11.5 7.6 %copy-start.6 = (f32[128]{0:T(128)S(1)}, f32[128]{0:T(128)}, u32[]{:S(2)}) copy-start(f32[128]{0:T(128)} %param.14) | copy-start | bytes 1540
  13.7 14.9 %all-to-all-start.1 = ((bf16[2,2,65536]{2,1,0:T(2,128)(2,1)}), bf16[2,2,65536]{2,1,0:T(2,128)(2,1)S(1)}, u32[]{:S(2)}, u32[]{:S(2)}) async-start(bf16[2,2,65536]{2,1,0:T(2,128)(2,1)} %convolution_convert_fusion), calls=%async_computation.1 | async-start | bytes 1048576 | tf_op jit(solution)/shard_map/all_to_all | solution.py:70
  19.2 6.5 %copy-start.7 = (s32[16]{0:T(128)S(1)}, s32[16]{0:T(128)}, u32[]{:S(2)}) copy-start(s32[16]{0:T(128)} %param.18) | copy-start | bytes 196
  28.6 18.3 %all-to-all-start = ((bf16[2,2,65536]{2,1,0:T(2,128)(2,1)}), bf16[2,2,65536]{2,1,0:T(2,128)(2,1)S(1)}, u32[]{:S(2)}, u32[]{:S(2)}) async-start(bf16[2,2,65536]{2,1,0:T(2,128)(2,1)} %convolution_convert_fusion.1), calls=%async_computation | async-start | bytes 1048576 | tf_op jit(solution)/shard_map/all_to_all | solution.py:71
